TPU v7x, 32 devices: a whole 2x2x4 slice. The times are simulated.
32 devices in a mesh: groups: 2 (over y), pool: 8 (over z, x), heads: 2 (over core).
Axes of the slice: x: 2, y: 2, z: 4, core: 2. Of those that a mesh axis runs over, the one named last changes fastest.
Arguments:
- hidden_in: bfloat16 [32, 8192], P('groups'), parts along dimension 0, may hold values from -50 to 50
- key_cache: bfloat16 [32, 8, 4096, 128], P('groups', 'heads', 'pool'), parts along dimension 0, may hold values from -200 to 200
- value_cache: bfloat16 [32, 8, 4096, 128], P('groups', 'heads', 'pool'), parts along dimension 0, may hold values from -6 to 6
- positions: int32 [3, 32, 4096], P(None, 'groups', 'pool'), parts along dimension 1, may hold values from 0 to 4095, as said below
- query_pos: int32 [3, 32], P(None, 'groups'), parts along dimension 1, may hold values from 4096 to 8207
- lengths: int32 [32], P('groups'), parts along dimension 0, may hold values from 1024 to 4096, as said below
- query_weight: bfloat16 [8192, 8192], P('pool', 'heads'), may hold values from -0.0625 to 0.0625
- key_weight: bfloat16 [8192, 1024], P('pool', 'heads'), may hold values from -0.16503906 to 0.16503906
- value_weight: bfloat16 [8192, 1024], P('pool', 'heads'), may hold values from -0.16503906 to 0.16503906
- out_weight: bfloat16 [8192, 8192], P('heads', 'pool'), may hold values from -0.5 to 0.5
- gate_weight: bfloat16 [8192, 14848], P(None, ('pool', 'heads')), may hold values from -0.0625 to 0.0625
- up_weight: bfloat16 [8192, 14848], P(None, ('pool', 'heads')), may hold values from -0.0625 to 0.0625
- down_weight: bfloat16 [14848, 8192], P(('pool', 'heads')), may hold values from -0.0625 to 0.0625
Outputs:
- output: bfloat16 [32, 8192], P('groups', 'pool'), parts along dimension 0
There are 2 independent parts, one for each index of `groups`. A program takes and returns all parts, laid end to end along the dimension named above; an argument that names none is the same for every part. Nothing has to cross between parts.
Inputs may be any that keep to these rules, and one draw needn't show every extreme that they name: `positions`: text tokens carry three equal ids; one prompt is text only. `lengths`: some prompt fills all 4096 slots.
All inputs are finite; a program needn't handle non-finite values.
Results may differ from a plain program's by a relative error of at most 0.007.
The roundings to bfloat16 on the way count: a program that leaves them out, or rounds other values in their place, can miss the bound.
Values may be sent and summed in bfloat16 or wider, within the bound.
A program may use at most 192 MiB of HBM per device.

v0:
```python
import math
import jax
import jax.numpy as jnp
from jax import lax
from jax.sharding import PartitionSpec as P

D = 8192
HEADS = 64
KV_HEADS = 8
HD = 128
PROMPTS = 16
EPS = 1e-06
THETA = 1000000.0


def angle_tables(triple):
    half_dim = HD // 2
    column = jnp.arange(half_dim)
    first_end = HD // 8
    second_end = first_end + 3 * HD // 16
    chosen = jnp.where(
        column < first_end,
        triple[0][..., None],
        jnp.where(column < second_end, triple[1][..., None], triple[2][..., None]),
    )
    inverse = jnp.exp(column.astype(jnp.float32) * (-2.0 * math.log(THETA) / HD))
    angles = chosen.astype(jnp.float32) * inverse
    return (jnp.cos(angles), jnp.sin(angles))


def rotate(values, cos_table, sin_table):
    half_dim = values.shape[-1] // 2
    lower_half = values[..., :half_dim]
    upper_half = values[..., half_dim:]
    return jnp.concatenate(
        [
            lower_half * cos_table - upper_half * sin_table,
            upper_half * cos_table + lower_half * sin_table,
        ],
        -1,
    )


def normalize(values):
    return values * lax.rsqrt(jnp.mean(values * values, -1, keepdims=True) + EPS)


def prepare(projected_rows, item_ids, local_heads, query_pos):
    query_width = projected_rows.shape[1] - 2 * HD
    prompt_ids = item_ids // local_heads
    triple = query_pos[:, prompt_ids]
    cos_table, sin_table = angle_tables(triple)
    item_count = projected_rows.shape[0]
    raw_queries = projected_rows[:, :query_width].reshape(item_count, query_width // HD, HD)
    queries = rotate(raw_queries, cos_table[:, None], sin_table[:, None]).astype(jnp.bfloat16)
    own_keys = rotate(
        projected_rows[:, query_width : query_width + HD], cos_table, sin_table
    ).astype(jnp.bfloat16)
    own_values = projected_rows[:, query_width + HD :].astype(jnp.bfloat16)
    return (queries, own_keys, own_values)


def partial_softmax(queries, key_rows, value_rows, item_lengths, offset):
    scores = jnp.einsum(
        "igd,isd->igs", queries, key_rows, preferred_element_type=jnp.float32
    ) * HD ** (-0.5)
    slot_index = offset + jnp.arange(key_rows.shape[1])
    valid_mask = slot_index[None, None, :] < item_lengths[:, None, None]
    scores = jnp.where(valid_mask, scores, -1e30)
    peak_score = jnp.max(scores, -1)
    weights = jnp.where(valid_mask, jnp.exp(scores - peak_score[..., None]), 0.0)
    weighted = jnp.einsum("igs,isd->igd", weights, value_rows.astype(jnp.float32))
    return (peak_score, jnp.sum(weights, -1), weighted.reshape(queries.shape[0], -1))


def combine(peaks, totals, weighted, own_score, own_values):
    item_count, source_count, group_size = peaks.shape
    top_score = jnp.maximum(jnp.max(peaks, 1), own_score)
    factor = jnp.exp(peaks - top_score[:, None])
    own_weight = jnp.exp(own_score - top_score)
    denominator = jnp.sum(totals * factor, 1) + own_weight
    numerator = jnp.sum(
        weighted.reshape(item_count, source_count, group_size, HD) * factor[..., None], 1
    )
    numerator = numerator + own_weight[..., None] * own_values.astype(jnp.float32)[:, None, :]
    return (
        (numerator / denominator[..., None])
        .reshape(item_count, group_size * HD)
        .astype(jnp.bfloat16)
    )


def per_device(
    hidden_in,
    key_cache,
    value_cache,
    positions,
    query_pos,
    lengths,
    query_weight,
    key_weight,
    value_weight,
    out_weight,
    gate_weight,
    up_weight,
    down_weight,
):
    pool_index = lax.axis_index("pool")
    pool_size = lax.axis_size("pool")
    local_heads = key_cache.shape[1]
    group_size = HEADS // KV_HEADS
    query_width = group_size * HD
    all_items = PROMPTS * local_heads
    my_count = all_items // pool_size
    my_start = pool_index * my_count
    seq_local = key_cache.shape[2]
    block_cols = D // pool_size
    normed = normalize(hidden_in.astype(jnp.float32)).astype(jnp.bfloat16)
    normed_cols = lax.dynamic_slice_in_dim(normed, pool_index * block_cols, block_cols, 1)
    term = jnp.concatenate(
        [
            jnp.dot(normed_cols, query_weight, preferred_element_type=jnp.float32).reshape(
                PROMPTS, local_heads, query_width
            ),
            jnp.dot(normed_cols, key_weight, preferred_element_type=jnp.float32).reshape(
                PROMPTS, local_heads, HD
            ),
            jnp.dot(normed_cols, value_weight, preferred_element_type=jnp.float32).reshape(
                PROMPTS, local_heads, HD
            ),
        ],
        2,
    ).reshape(all_items, query_width + 2 * HD)
    cos_table, sin_table = angle_tables(positions)
    rotated = rotate(key_cache.astype(jnp.float32), cos_table[:, None], sin_table[:, None]).astype(
        jnp.bfloat16
    )
    rotated = rotated.reshape(all_items, seq_local, HD)
    value_rows = value_cache.reshape(all_items, seq_local, HD)
    item_lengths = jnp.repeat(lengths, local_heads)
    projected_all = lax.psum(term, "pool")
    all_queries, all_keys, all_values = prepare(
        projected_all, jnp.arange(all_items), local_heads, query_pos
    )
    local_peaks, local_totals, local_weighted = partial_softmax(
        all_queries, rotated, value_rows, item_lengths, pool_index * seq_local
    )
    peaks, totals, weighted = (
        lax.all_to_all(local_peaks[:, None], "pool", split_axis=0, concat_axis=1, tiled=True),
        lax.all_to_all(local_totals[:, None], "pool", split_axis=0, concat_axis=1, tiled=True),
        lax.all_to_all(local_weighted[:, None], "pool", split_axis=0, concat_axis=1, tiled=True),
    )
    queries = lax.dynamic_slice_in_dim(all_queries, my_start, my_count, 0)
    own_keys = lax.dynamic_slice_in_dim(all_keys, my_start, my_count, 0)
    own_values = lax.dynamic_slice_in_dim(all_values, my_start, my_count, 0)
    own_score = jnp.einsum(
        "igd,id->ig", queries, own_keys, preferred_element_type=jnp.float32
    ) * HD ** (-0.5)
    attended = combine(peaks, totals, weighted, own_score, own_values)
    gathered = lax.all_gather(attended, "pool", axis=0, tiled=True).reshape(
        PROMPTS, local_heads * query_width
    )
    attn_out = lax.psum(jnp.dot(gathered, out_weight, preferred_element_type=jnp.float32), "heads")
    hidden_cols = lax.dynamic_slice_in_dim(hidden_in, pool_index * block_cols, block_cols, 1)
    mid_state = (hidden_cols.astype(jnp.float32) + attn_out).astype(jnp.bfloat16)
    squares = lax.psum(jnp.sum(jnp.square(mid_state.astype(jnp.float32)), -1), "pool")
    whole_state = lax.all_gather(mid_state, "pool", axis=1, tiled=True)
    inverse = lax.rsqrt(squares / D + EPS)
    normed_state = (whole_state.astype(jnp.float32) * inverse[:, None]).astype(jnp.bfloat16)
    gate_values = jnp.dot(normed_state, gate_weight, preferred_element_type=jnp.float32)
    up_values = jnp.dot(normed_state, up_weight, preferred_element_type=jnp.float32)
    active = (jax.nn.silu(gate_values) * up_values).astype(jnp.bfloat16)
    partial_out = jnp.dot(active, down_weight, preferred_element_type=jnp.float32)
    mlp_cols = lax.psum_scatter(partial_out, "pool", scatter_dimension=1, tiled=True)
    mlp_cols = lax.psum(mlp_cols, "heads")
    return (mid_state.astype(jnp.float32) + mlp_cols).astype(jnp.bfloat16)


def solution(mesh):
    in_specs = (
        P("groups", None),
        P("groups", "heads", "pool", None),
        P("groups", "heads", "pool", None),
        P(None, "groups", "pool"),
        P(None, "groups"),
        P("groups"),
        P("pool", "heads"),
        P("pool", "heads"),
        P("pool", "heads"),
        P("heads", "pool"),
        P(None, ("pool", "heads")),
        P(None, ("pool", "heads")),
        P(("pool", "heads"), None),
    )
    out_specs = P("groups", "pool")
    return jax.shard_map(
        per_device, mesh=mesh, in_specs=in_specs, out_specs=out_specs, check_vma=False
    )
```

profile of v0, /device:TPU:0, one launch (start us, length us, event | category | flops | bytes accessed | tf_op | source)
XLA Modules:
  0.0 357.5 jit_solution(8407712216756091066)
XLA Ops:
  6.5 1.1 convert_element_type.78
  7.6 1.1 multiply_reduce_fusion
  9.1 1.5 fusion.50
  10.6 4.6 %fusion.52 = f32[16,4096]{1,0:T(8,128)S(1)} fusion(bf16[1024,4096]{1,0:T(8,128)(2,1)} %param.19, f32[16,8192]{1,0:T(8,128)S(1)} %convert_element_type.78, s32[]{:T(128)S(6)} %select_n.82, f32[16]{0:T(128)S(1)} %add_rsqrt_fusion.1), kind=kOutput, calls=%fused_computation.96 | convolution fusion | flops 134250496 | bytes 8716804 | tf_op jit(solution)/shard_map/dot_general | solution.py:122
  15.3 0.7 pad_maximum_fusion
  16.1 11.3 %convert_element_type.82 = f32[16,4,512,128]{3,2,1,0:T(8,128)} convert(bf16[16,4,512,128]{3,2,1,0:T(8,128)(2,1)} %param.14) | non-fusion elementwise | flops 4194304 | bytes 25165824 | tf_op jit(solution)/shard_map/convert_element_type | solution.py:135
  27.6 0.6 gather_fusion
  28.5 42.2 %fusion.5 = (f32[16,512,64]{2,1,0:T(8,128)S(1)}, f32[16,512,64]{2,1,0:T(8,128)S(1)}) fusion(f32[64]{0:T(128)S(1)} %multiply_exponential_fusion, s32[16,512]{1,0:T(8,128)S(1)} %get-tuple-element.23, s32[16,512]{1,0:T(8,128)S(1)} %get-tuple-element.24, s32[16,512]{1,0:T(8,128)S(1)} %get-tuple-element.22, pred[64]{0:T(512)(128)(4,1)S(1)} %get-tuple-element.29, ...), kind=kLoop, calls=%fused_computation.9 | loop fusion | flops 2097152 | bytes 4292992 | tf_op jit(solution)/shard_map/cos | solution.py:28
  70.7 19.2 %subtract_convert_fusion = (bf16[16,4,512,64]{3,2,1,0:T(8,128)(2,1)}, bf16[16,4,512,64]{3,2,1,0:T(8,128)(2,1)}) fusion(f32[16,4,512,128]{3,2,1,0:T(8,128)} %convert_element_type.82, f32[16,512,64]{2,1,0:T(8,128)S(1)} %get-tuple-element.21, f32[16,512,64]{2,1,0:T(8,128)S(1)} %get-tuple-element.20), kind=kLoop, calls=%fused_computation.2 | loop fusion | flops 16777216 | bytes 29360128 | tf_op jit(solution)/shard_map/convert.6
  90.3 1.0 slice_bitcast_fusion
  91.3 1.1 subtract_convert_fusion.2
  92.6 9.3 %fusion.49 = (f32[64,8]{1,0:T(8,128)}, f32[64,8,512]{2,1,0:T(8,128)S(1)}) fusion(bf16[64,512,64]{2,1,0:T(8,128)(2,1)} %bitcast.54, bf16[64,512,64]{2,1,0:T(8,128)(2,1)} %bitcast.53, bf16[64,8,64]{2,1,0:T(8,128)(2,1)S(1)} %get-tuple-element.19, bf16[64,8,64]{2,1,0:T(8,128)(2,1)S(1)} %get-tuple-element.18, pred[64,512]{1,0:T(8,128)(4,1)S(1)} %broadcast_compare_fusion), kind=kOutput, calls=%fused_computation.94 | convolution fusion | flops 84934144 | bytes 9603072 | tf_op jit(solution)/shard_map/igd,isd->igs/dot_general | solution.py:64
  101.9 7.1 %all-to-all-start.1 = ((f32[64,1,8]{2,1,0:T(1,128)}), f32[64,1,8]{2,1,0:T(1,128)S(1)}, u32[]{:S(2)}, u32[]{:S(2)}) async-start(f32[64,1,8]{2,1,0:T(1,128)} %bitcast.11), calls=%async_computation.1 | async-start | bytes 65536 | tf_op jit(solution)/shard_map/all_to_all | solution.py:149
  109.2 5.4 %fusion.14 = f32[64,8,128]{2,1,0:T(8,128)} fusion(bf16[64,512,128]{2,1,0:T(8,128)(2,1)} %bitcast.55, f32[64,8,512]{2,1,0:T(8,128)S(1)} %get-tuple-element.28, f32[64,8]{1,0:T(8,128)} %get-tuple-element.27, pred[64,512]{1,0:T(8,128)(4,1)S(1)} %broadcast_compare_fusion), kind=kOutput, calls=%fused_computation.16 | convolution fusion | flops 67633152 | bytes 9734144 | tf_op jit(solution)/shard_map/igs,isd->igd/dot_general | solution.py:72
  114.5 1.7 fusion.13
  116.3 0.8 slice.72
  117.1 6.0 %all-to-all-start.2 = ((f32[64,1,8]{2,1,0:T(1,128)}), f32[64,1,8]{2,1,0:T(1,128)S(1)}, u32[]{:S(2)}, u32[]{:S(2)}) async-start(f32[64,1,8]{2,1,0:T(1,128)} %bitcast.21), calls=%async_computation.2 | async-start | bytes 65536 | tf_op jit(solution)/shard_map/all_to_all | solution.py:150
  123.1 6.7 %all-to-all-done.2 = f32[64,1,8]{2,1,0:T(1,128)S(1)} async-done(((f32[64,1,8]{2,1,0:T(1,128)}), f32[64,1,8]{2,1,0:T(1,128)S(1)}, u32[]{:S(2)}, u32[]{:S(2)}) %all-to-all-start.2) | async-done | bytes 2080 | tf_op jit(solution)/shard_map/all_to_all | solution.py:150
  129.7 3.4 all-to-all-start
  133.4 7.9 %all-to-all-done = f32[64,1,1024]{2,1,0:T(1,128)S(1)} async-done(((f32[64,1,1024]{2,1,0:T(1,128)}), f32[64,1,1024]{2,1,0:T(1,128)S(1)}, u32[]{:S(2)}, u32[]{:S(2)}) %all-to-all-start) | async-done | bytes 262176 | tf_op jit(solution)/shard_map/all_to_all | solution.py:151
  141.4 0.4 multiply_reduce_fusion.1
  141.9 30.6 %all_gather.6 = bf16[64,1024]{1,0:T(8,128)(2,1)S(1)} all-gather(bf16[8,1024]{1,0:T(8,128)(2,1)S(1)} %fusion.31), channel_id=1, replica_groups=mesh['groups'=2,'pool'=8,'heads'=2] {'pool'}, dimensions={0}, use_global_device_ids=true | all-gather | bytes 147456 | tf_op jit(solution)/shard_map/all_gather | solution.py:160
  172.6 5.2 %fusion.56 = f32[16,1024]{1,0:T(8,128)} fusion(bf16[16,4096]{1,0:T(8,128)(2,1)S(1)} %reshape.304, bf16[4096,1024]{1,0:T(8,128)(2,1)} %param.22), kind=kOutput, calls=%fused_computation.98 | convolution fusion | flops 134217728 | bytes 8585216 | tf_op jit(solution)/shard_map/dot_general | solution.py:163
  177.8 16.1 %all-reduce.6.cloned.1.call-done = f32[16,1024]{1,0:T(8,128)} async-done(((f32[16,1024]{1,0:T(8,128)}), f32[16,1024]{1,0:T(8,128)}) %all-reduce.6.cloned.1.call-update) | async-done | bytes 65552 | tf_op jit(solution)/shard_map/psum | solution.py:163
  193.9 1.0 fusion.23
  194.9 31.1 %all_gather.7 = bf16[16,8192]{1,0:T(8,128)(2,1)S(1)} all-gather(bf16[16,1024]{1,0:T(8,128)(2,1)S(1)} %get-tuple-element.9), channel_id=1, replica_groups=mesh['groups'=2,'pool'=8,'heads'=2] {'pool'}, dimensions={1}, use_global_device_ids=true | all-gather | bytes 294912 | tf_op jit(solution)/shard_map/all_gather | solution.py:167
  226.0 21.3 %psum.30 = f32[16]{0:T(128)S(1)} all-reduce(f32[16]{0:T(128)S(1)} %get-tuple-element.8), channel_id=1, replica_groups=mesh['groups'=2,'pool'=8,'heads'=2] {'pool'}, use_global_device_ids=true, to_apply=%region_9.10 | all-reduce | flops 16 | bytes 128 | tf_op jit(solution)/shard_map/psum | solution.py:166
  247.3 9.4 %fusion.22 = f32[16,928]{1,0:T(8,128)S(1)} fusion(bf16[8192,928]{0,1:T(8,128)(2,1)} %param.23, bf16[16,8192]{1,0:T(8,128)(2,1)S(1)} %all_gather.7, f32[16]{0:T(128)S(1)} %add_rsqrt_fusion), kind=kOutput, calls=%fused_computation.33 | convolution fusion | flops 243662848 | bytes 15525952 | tf_op jit(solution)/shard_map/dot_general | solution.py:170
  256.7 13.9 %fusion.15 = f32[16,8192]{1,0:T(8,128)} fusion(bf16[928,8192]{1,0:T(8,128)(2,1)} %param.25, bf16[8192,928]{0,1:T(8,128)(2,1)} %param.24, bf16[16,8192]{1,0:T(8,128)(2,1)S(1)} %all_gather.7, f32[16]{0:T(128)S(1)} %add_rsqrt_fusion, f32[16,928]{1,0:T(8,128)S(1)} %fusion.22), kind=kOutput, calls=%fused_computation.17 | convolution fusion | flops 487021568 | bytes 31254592 | tf_op jit(solution)/shard_map/dot_general | solution.py:173
  270.7 60.0 %reduce-scatter.2.cloned.1.call-done = f32[16,1024]{1,0:T(8,128)} async-done(((f32[16,8192]{1,0:T(8,128)}), f32[16,1024]{1,0:T(8,128)}) %reduce-scatter.2.cloned.1.call-update) | async-done | bytes 65552 | tf_op jit(solution)/shard_map/reduce_scatter | solution.py:174
  330.7 18.8 %all-reduce.8.cloned.1.call-done = f32[16,1024]{1,0:T(8,128)} async-done(((f32[16,1024]{1,0:T(8,128)}), f32[16,1024]{1,0:T(8,128)}) %all-reduce.8.cloned.1.call-update) | async-done | bytes 65552 | tf_op jit(solution)/shard_map/psum | solution.py:175
  349.5 1.5 fusion.24
  (51 shorter events, 2.4 us)
Async XLA Ops:
  6.5 2.2 copy-start
  6.5 83.8 %all-reduce.4.cloned.1.call-start = ((), (), s32[]{:S(2)}) async-start(), calls=%async_computation.4 | async-start | bytes 655360 | tf_op jit(solution)/shard_map/psum | solution.py:141
  16.1 11.4 %copy-start.2 = (s32[3,16,512]{2,1,0:T(8,128)S(1)}, s32[3,16,512]{2,1,0:T(8,128)}, u32[]{:S(2)}) copy-start(s32[3,16,512]{2,1,0:T(8,128)} %param.16) | copy-start | bytes 294916
  16.1 11.4 %copy-start.3 = (s32[3,16]{1,0:T(4,128)S(1)}, s32[3,16]{1,0:T(4,128)}, u32[]{:S(2)}) copy-start(s32[3,16]{1,0:T(4,128)} %param.17) | copy-start | bytes 580
  16.1 12.2 %copy-start.4 = (s32[16]{0:T(128)S(1)}, s32[16]{0:T(128)}, u32[]{:S(2)}) copy-start(s32[16]{0:T(128)} %param.18) | copy-start | bytes 196
  101.9 15.2 %all-to-all-start.1 = ((f32[64,1,8]{2,1,0:T(1,128)}), f32[64,1,8]{2,1,0:T(1,128)S(1)}, u32[]{:S(2)}, u32[]{:S(2)}) async-start(f32[64,1,8]{2,1,0:T(1,128)} %bitcast.11), calls=%async_computation.1 | async-start | bytes 65536 | tf_op jit(solution)/shard_map/all_to_all | solution.py:149
  117.1 12.7 %all-to-all-start.2 = ((f32[64,1,8]{2,1,0:T(1,128)}), f32[64,1,8]{2,1,0:T(1,128)S(1)}, u32[]{:S(2)}, u32[]{:S(2)}) async-start(f32[64,1,8]{2,1,0:T(1,128)} %bitcast.21), calls=%async_computation.2 | async-start | bytes 65536 | tf_op jit(solution)/shard_map/all_to_all | solution.py:150
  129.7 11.6 %all-to-all-start = ((f32[64,1,1024]{2,1,0:T(1,128)}), f32[64,1,1024]{2,1,0:T(1,128)S(1)}, u32[]{:S(2)}, u32[]{:S(2)}) async-start(f32[64,1,1024]{2,1,0:T(1,128)} %bitcast.8), calls=%async_computation | async-start | bytes 524288 | tf_op jit(solution)/shard_map/all_to_all | solution.py:151
  133.2 60.8 %all-reduce.6.cloned.1.call-start = ((), (), s32[]{:S(2)}) async-start(), calls=%async_computation.5 | async-start | bytes 131072 | tf_op jit(solution)/shard_map/psum | solution.py:163
  177.8 152.9 %reduce-scatter.2.cloned.1.call-start = ((), (), s32[]{:S(2)}) async-start(), calls=%async_computation.6 | async-start | bytes 589824 | tf_op jit(solution)/shard_map/reduce_scatter | solution.py:174
  247.3 103.7 %copy-start.1 = (bf16[1024,512]{1,0:T(8,128)(2,1)S(1)}, bf16[1024,512]{1,0:T(8,128)(2,1)}, u32[]{:S(2)}) copy-start(bf16[1024,512]{1,0:T(8,128)(2,1)} %param.21) | copy-start | bytes 3145732
  270.7 78.9 %all-reduce.8.cloned.1.call-start = ((), (), s32[]{:S(2)}) async-start(), calls=%async_computation.7 | async-start | bytes 131072 | tf_op jit(solution)/shard_map/psum | solution.py:175
Sparse Core Ops, SparseCore 0:
  16.2 74.0 all-reduce.3
  177.9 15.9 all-reduce.5
  270.8 59.8 reduce-scatter.1
  332.8 16.6 all-reduce.7
where the time goes:
time: 358 us
  waiting for transfers between devices  110 us (31%)
  blocking collectives  82.9 us (23%)
  other arithmetic  81.8 us (23%)
  matrix products  49.8 us (14%)
  starting transfers between devices  16.6 us (5%)
  between operations  13.3 us (4%)
    reduce_scatter x1, waiting for transfers between devices, per_device(): lax.psum_scatter(partial_out, 'pool', scatter_dimension=1, tiled=True)  60 us
    cos x1, other arithmetic, angle_tables(): return (jnp.cos(angles), jnp.sin(angles))  42.2 us
    all_gather x1, blocking collectives, per_device(): whole_state = lax.all_gather(mid_state, 'pool', axis=1, tiled=True)  31.1 us
    all_gather x1, blocking collectives, per_device(): lax.all_gather(attended, 'pool', axis=0, tiled=True)  30.6 us
    psum x1, blocking collectives, per_device(): lax.psum(jnp.sum(jnp.square(mid_state.astype(jnp.float32)), -1), 'pool')  21.3 us
    another operation x3, other arithmetic  20.5 us
    psum x1, waiting for transfers between devices, per_device(): mlp_cols = lax.psum(mlp_cols, 'heads')  18.8 us
    psum x1, waiting for transfers between devices, per_device(): lax.psum(jnp.dot(gathered, out_weight, preferred_element_type=jnp.float32...  16.1 us
  transfers between devices with their start and end apart: 7, of which 6 were waited for; matrix products, arithmetic and copies ran while one was open for 23% of the time, Pallas kernels for 0%

commit v1 on v0

--- a/solution.py
+++ b/solution.py
@@ -172,7 +172,7 @@
     active = (jax.nn.silu(gate_values) * up_values).astype(jnp.bfloat16)
     partial_out = jnp.dot(active, down_weight, preferred_element_type=jnp.float32)
     mlp_cols = lax.psum_scatter(partial_out, "pool", scatter_dimension=1, tiled=True)
-    mlp_cols = lax.psum(mlp_cols, "heads")
+    mlp_cols = lax.all_gather(mlp_cols, "heads").sum(axis=0)
     return (mid_state.astype(jnp.float32) + mlp_cols).astype(jnp.bfloat16)
 
 

time: 358 us -> 341 us (0.953)
  waiting for transfers between devices: 110 us -> 91 us
    psum x1 -> x0, waiting for transfers between devices: 18.8 us -> none  [per_device(): mlp_cols = lax.psum(mlp_cols, 'heads')]
  transfers between devices with their start and end apart: 7 -> 6, of which waited for: 6 -> 5; matrix products, arithmetic and copies ran while one was open for 23% -> 24% of each run, Pallas kernels for 0% -> 0%
where the time goes in v1:
time: 341 us; the launch traced here: 340 us
  waiting for transfers between devices  91 us (27%)
  blocking collectives  85 us (25%)
  other arithmetic  81 us (24%)
  matrix products  49.8 us (15%)
  starting transfers between devices  16.6 us (5%)
  between operations  13.3 us (4%)
    reduce_scatter x1, waiting for transfers between devices, per_device(): lax.psum_scatter(partial_out, 'pool', scatter_dimension=1, tiled=True)  60 us
    cos x1, other arithmetic, angle_tables(): return (jnp.cos(angles), jnp.sin(angles))  42.2 us
    all_gather x1, blocking collectives, per_device(): whole_state = lax.all_gather(mid_state, 'pool', axis=1, tiled=True)  31.1 us
    all_gather x1, blocking collectives, per_device(): lax.all_gather(attended, 'pool', axis=0, tiled=True)  30.6 us
    psum x1, blocking collectives, per_device(): lax.psum(jnp.sum(jnp.square(mid_state.astype(jnp.float32)), -1), 'pool')  21.3 us
    another operation x3, other arithmetic  20.5 us
    psum x1, waiting for transfers between devices, per_device(): lax.psum(jnp.dot(gathered, out_weight, preferred_element_type=jnp.float32...  16.1 us
    dot_general x1, matrix products, per_device(): jnp.dot(active, down_weight, preferred_element_type=jnp.float32)  13.9 us
  transfers between devices with their start and end apart: 6, of which 5 were waited for; matrix products, arithmetic and copies ran while one was open for 24% of the time, Pallas kernels for 0%

profile of v1, /device:TPU:0, one launch (start us, length us, event | category | flops | bytes accessed | tf_op | source)
XLA Modules:
  0.0 339.9 jit_solution(11020386325790482395)
XLA Ops:
  6.5 1.1 convert_element_type.78
  7.6 1.1 multiply_reduce_fusion
  9.1 1.5 fusion.50
  10.6 4.6 %fusion.52 = f32[16,4096]{1,0:T(8,128)S(1)} fusion(bf16[1024,4096]{1,0:T(8,128)(2,1)} %param.19, f32[16,8192]{1,0:T(8,128)S(1)} %convert_element_type.78, s32[]{:T(128)S(6)} %select_n.82, f32[16]{0:T(128)S(1)} %add_rsqrt_fusion.1), kind=kOutput, calls=%fused_computation.96 | convolution fusion | flops 134250496 | bytes 8716804 | tf_op jit(solution)/shard_map/dot_general | solution.py:122
  15.3 0.7 pad_maximum_fusion
  16.1 11.3 %convert_element_type.82 = f32[16,4,512,128]{3,2,1,0:T(8,128)} convert(bf16[16,4,512,128]{3,2,1,0:T(8,128)(2,1)} %param.14) | non-fusion elementwise | flops 4194304 | bytes 25165824 | tf_op jit(solution)/shard_map/convert_element_type | solution.py:135
  27.6 0.6 gather_fusion
  28.5 42.2 %fusion.5 = (f32[16,512,64]{2,1,0:T(8,128)S(1)}, f32[16,512,64]{2,1,0:T(8,128)S(1)}) fusion(f32[64]{0:T(128)S(1)} %multiply_exponential_fusion, s32[16,512]{1,0:T(8,128)S(1)} %get-tuple-element.23, s32[16,512]{1,0:T(8,128)S(1)} %get-tuple-element.24, s32[16,512]{1,0:T(8,128)S(1)} %get-tuple-element.22, pred[64]{0:T(512)(128)(4,1)S(1)} %get-tuple-element.29, ...), kind=kLoop, calls=%fused_computation.9 | loop fusion | flops 2097152 | bytes 4292992 | tf_op jit(solution)/shard_map/cos | solution.py:28
  70.7 19.2 %subtract_convert_fusion = (bf16[16,4,512,64]{3,2,1,0:T(8,128)(2,1)}, bf16[16,4,512,64]{3,2,1,0:T(8,128)(2,1)}) fusion(f32[16,4,512,128]{3,2,1,0:T(8,128)} %convert_element_type.82, f32[16,512,64]{2,1,0:T(8,128)S(1)} %get-tuple-element.21, f32[16,512,64]{2,1,0:T(8,128)S(1)} %get-tuple-element.20), kind=kLoop, calls=%fused_computation.2 | loop fusion | flops 16777216 | bytes 29360128 | tf_op jit(solution)/shard_map/convert.6
  90.3 1.0 slice_bitcast_fusion
  91.3 1.1 subtract_convert_fusion.2
  92.6 9.3 %fusion.49 = (f32[64,8]{1,0:T(8,128)}, f32[64,8,512]{2,1,0:T(8,128)S(1)}) fusion(bf16[64,512,64]{2,1,0:T(8,128)(2,1)} %bitcast.55, bf16[64,512,64]{2,1,0:T(8,128)(2,1)} %bitcast.54, bf16[64,8,64]{2,1,0:T(8,128)(2,1)S(1)} %get-tuple-element.19, bf16[64,8,64]{2,1,0:T(8,128)(2,1)S(1)} %get-tuple-element.18, pred[64,512]{1,0:T(8,128)(4,1)S(1)} %broadcast_compare_fusion), kind=kOutput, calls=%fused_computation.94 | convolution fusion | flops 84934144 | bytes 9603072 | tf_op jit(solution)/shard_map/igd,isd->igs/dot_general | solution.py:64
  101.9 7.1 %all-to-all-start.1 = ((f32[64,1,8]{2,1,0:T(1,128)}), f32[64,1,8]{2,1,0:T(1,128)S(1)}, u32[]{:S(2)}, u32[]{:S(2)}) async-start(f32[64,1,8]{2,1,0:T(1,128)} %bitcast.11), calls=%async_computation.1 | async-start | bytes 65536 | tf_op jit(solution)/shard_map/all_to_all | solution.py:149
  109.2 5.4 %fusion.14 = f32[64,8,128]{2,1,0:T(8,128)} fusion(bf16[64,512,128]{2,1,0:T(8,128)(2,1)} %bitcast.56, f32[64,8,512]{2,1,0:T(8,128)S(1)} %get-tuple-element.28, f32[64,8]{1,0:T(8,128)} %get-tuple-element.27, pred[64,512]{1,0:T(8,128)(4,1)S(1)} %broadcast_compare_fusion), kind=kOutput, calls=%fused_computation.16 | convolution fusion | flops 67633152 | bytes 9734144 | tf_op jit(solution)/shard_map/igs,isd->igd/dot_general | solution.py:72
  114.5 1.7 fusion.13
  116.3 0.8 slice.72
  117.1 6.0 %all-to-all-start.2 = ((f32[64,1,8]{2,1,0:T(1,128)}), f32[64,1,8]{2,1,0:T(1,128)S(1)}, u32[]{:S(2)}, u32[]{:S(2)}) async-start(f32[64,1,8]{2,1,0:T(1,128)} %bitcast.21), calls=%async_computation.2 | async-start | bytes 65536 | tf_op jit(solution)/shard_map/all_to_all | solution.py:150
  123.1 6.7 %all-to-all-done.2 = f32[64,1,8]{2,1,0:T(1,128)S(1)} async-done(((f32[64,1,8]{2,1,0:T(1,128)}), f32[64,1,8]{2,1,0:T(1,128)S(1)}, u32[]{:S(2)}, u32[]{:S(2)}) %all-to-all-start.2) | async-done | bytes 2080 | tf_op jit(solution)/shard_map/all_to_all | solution.py:150
  129.7 3.4 %all-to-all-start = ((f32[64,1,1024]{2,1,0:T(1,128)}), f32[64,1,1024]{2,1,0:T(1,128)S(1)}, u32[]{:S(2)}, u32[]{:S(2)}) async-start(f32[64,1,1024]{2,1,0:T(1,128)} %bitcast.8), calls=%async_computation | async-start | bytes 524288 | tf_op jit(solution)/shard_map/all_to_all | solution.py:151
  133.4 7.9 %all-to-all-done = f32[64,1,1024]{2,1,0:T(1,128)S(1)} async-done(((f32[64,1,1024]{2,1,0:T(1,128)}), f32[64,1,1024]{2,1,0:T(1,128)S(1)}, u32[]{:S(2)}, u32[]{:S(2)}) %all-to-all-start) | async-done | bytes 262176 | tf_op jit(solution)/shard_map/all_to_all | solution.py:151
  141.4 0.4 multiply_reduce_fusion.1
  141.9 30.6 %all_gather.12 = bf16[64,1024]{1,0:T(8,128)(2,1)S(1)} all-gather(bf16[8,1024]{1,0:T(8,128)(2,1)S(1)} %fusion.31), channel_id=1, replica_groups=mesh['groups'=2,'pool'=8,'heads'=2] {'pool'}, dimensions={0}, use_global_device_ids=true | all-gather | bytes 147456 | tf_op jit(solution)/shard_map/all_gather | solution.py:160
  172.6 5.2 %fusion.56 = f32[16,1024]{1,0:T(8,128)} fusion(bf16[16,4096]{1,0:T(8,128)(2,1)S(1)} %reshape.304, bf16[4096,1024]{1,0:T(8,128)(2,1)} %param.22), kind=kOutput, calls=%fused_computation.98 | convolution fusion | flops 134217728 | bytes 8585216 | tf_op jit(solution)/shard_map/dot_general | solution.py:163
  177.8 16.1 %all-reduce.5.cloned.1.call-done = f32[16,1024]{1,0:T(8,128)} async-done(((f32[16,1024]{1,0:T(8,128)}), f32[16,1024]{1,0:T(8,128)}) %all-reduce.5.cloned.1.call-update) | async-done | bytes 65552 | tf_op jit(solution)/shard_map/psum | solution.py:163
  193.9 1.0 fusion.23
  194.9 31.1 %all_gather.13 = bf16[16,8192]{1,0:T(8,128)(2,1)S(1)} all-gather(bf16[16,1024]{1,0:T(8,128)(2,1)S(1)} %get-tuple-element.9), channel_id=1, replica_groups=mesh['groups'=2,'pool'=8,'heads'=2] {'pool'}, dimensions={1}, use_global_device_ids=true | all-gather | bytes 294912 | tf_op jit(solution)/shard_map/all_gather | solution.py:167
  226.0 21.3 %psum.23 = f32[16]{0:T(128)S(1)} all-reduce(f32[16]{0:T(128)S(1)} %get-tuple-element.8), channel_id=1, replica_groups=mesh['groups'=2,'pool'=8,'heads'=2] {'pool'}, use_global_device_ids=true, to_apply=%region_9.10 | all-reduce | flops 16 | bytes 128 | tf_op jit(solution)/shard_map/psum | solution.py:166
  247.3 9.4 %fusion.22 = f32[16,928]{1,0:T(8,128)S(1)} fusion(bf16[8192,928]{0,1:T(8,128)(2,1)} %param.23, bf16[16,8192]{1,0:T(8,128)(2,1)S(1)} %all_gather.13, f32[16]{0:T(128)S(1)} %add_rsqrt_fusion), kind=kOutput, calls=%fused_computation.33 | convolution fusion | flops 243662848 | bytes 15525952 | tf_op jit(solution)/shard_map/dot_general | solution.py:170
  256.7 13.9 %fusion.15 = f32[16,8192]{1,0:T(8,128)} fusion(bf16[928,8192]{1,0:T(8,128)(2,1)} %param.25, bf16[8192,928]{0,1:T(8,128)(2,1)} %param.24, bf16[16,8192]{1,0:T(8,128)(2,1)S(1)} %all_gather.13, f32[16]{0:T(128)S(1)} %add_rsqrt_fusion, f32[16,928]{1,0:T(8,128)S(1)} %fusion.22), kind=kOutput, calls=%fused_computation.17 | convolution fusion | flops 487021568 | bytes 31254592 | tf_op jit(solution)/shard_map/dot_general | solution.py:173
  270.7 60.0 %reduce-scatter.2.cloned.1.call-done = f32[16,1024]{1,0:T(8,128)} async-done(((f32[16,8192]{1,0:T(8,128)}), f32[16,1024]{1,0:T(8,128)}) %reduce-scatter.2.cloned.1.call-update) | async-done | bytes 65552 | tf_op jit(solution)/shard_map/reduce_scatter | solution.py:174
  330.7 2.1 all-gather
  332.8 0.6 fusion.24
  (50 shorter events, 2.3 us)
Async XLA Ops:
  6.5 2.2 copy-start
  6.5 83.8 %all-reduce.3.cloned.1.call-start = ((), (), s32[]{:S(2)}) async-start(), calls=%async_computation.4 | async-start | bytes 655360 | tf_op jit(solution)/shard_map/psum | solution.py:141
  16.1 11.4 %copy-start.2 = (s32[3,16,512]{2,1,0:T(8,128)S(1)}, s32[3,16,512]{2,1,0:T(8,128)}, u32[]{:S(2)}) copy-start(s32[3,16,512]{2,1,0:T(8,128)} %param.16) | copy-start | bytes 294916
  16.1 11.4 %copy-start.3 = (s32[3,16]{1,0:T(4,128)S(1)}, s32[3,16]{1,0:T(4,128)}, u32[]{:S(2)}) copy-start(s32[3,16]{1,0:T(4,128)} %param.17) | copy-start | bytes 580
  16.1 12.2 %copy-start.4 = (s32[16]{0:T(128)S(1)}, s32[16]{0:T(128)}, u32[]{:S(2)}) copy-start(s32[16]{0:T(128)} %param.18) | copy-start | bytes 196
  101.9 15.2 %all-to-all-start.1 = ((f32[64,1,8]{2,1,0:T(1,128)}), f32[64,1,8]{2,1,0:T(1,128)S(1)}, u32[]{:S(2)}, u32[]{:S(2)}) async-start(f32[64,1,8]{2,1,0:T(1,128)} %bitcast.11), calls=%async_computation.1 | async-start | bytes 65536 | tf_op jit(solution)/shard_map/all_to_all | solution.py:149
  117.1 12.7 %all-to-all-start.2 = ((f32[64,1,8]{2,1,0:T(1,128)}), f32[64,1,8]{2,1,0:T(1,128)S(1)}, u32[]{:S(2)}, u32[]{:S(2)}) async-start(f32[64,1,8]{2,1,0:T(1,128)} %bitcast.21), calls=%async_computation.2 | async-start | bytes 65536 | tf_op jit(solution)/shard_map/all_to_all | solution.py:150
  129.7 11.6 %all-to-all-start = ((f32[64,1,1024]{2,1,0:T(1,128)}), f32[64,1,1024]{2,1,0:T(1,128)S(1)}, u32[]{:S(2)}, u32[]{:S(2)}) async-start(f32[64,1,1024]{2,1,0:T(1,128)} %bitcast.8), calls=%async_computation | async-start | bytes 524288 | tf_op jit(solution)/shard_map/all_to_all | solution.py:151
  133.2 60.8 %all-reduce.5.cloned.1.call-start = ((), (), s32[]{:S(2)}) async-start(), calls=%async_computation.5 | async-start | bytes 131072 | tf_op jit(solution)/shard_map/psum | solution.py:163
  177.8 152.9 %reduce-scatter.2.cloned.1.call-start = ((), (), s32[]{:S(2)}) async-start(), calls=%async_computation.6 | async-start | bytes 589824 | tf_op jit(solution)/shard_map/reduce_scatter | solution.py:174
  247.3 86.1 %copy-start.1 = (bf16[1024,512]{1,0:T(8,128)(2,1)S(1)}, bf16[1024,512]{1,0:T(8,128)(2,1)}, u32[]{:S(2)}) copy-start(bf16[1024,512]{1,0:T(8,128)(2,1)} %param.21) | copy-start | bytes 3145732
Sparse Core Ops, SparseCore 0:
  16.2 74.0 all-reduce.2
  177.9 15.9 all-reduce.4
  270.8 59.8 reduce-scatter.1
